TPU v7x, 128 devices: a whole 4x4x4 slice. The times are simulated.
128 devices in a mesh: enc: 32 (over z, x, core), llm: 4 (over y).
Axes of the slice: x: 4, y: 4, z: 4, core: 2. Of those that a mesh axis runs over, the one named last changes fastest.
Arguments:
- patches: bfloat16 [16384, 5120], P('enc', 'llm'), may hold values from -6 to 6
- ln_gain: bfloat16 [1280], replicated, may hold values from 0.099609375 to 1.8984375
- w_in: bfloat16 [5120, 5120], P(None, 'llm'), may hold values from -0.078125 to 0.078125
- b_in: bfloat16 [5120], P('llm'), may hold values from -3 to 3
- w_out: bfloat16 [5120, 2048], P('llm'), may hold values from -0.078125 to 0.078125
- b_out: bfloat16 [2048], replicated, may hold values from -3 to 3
- owner: int32 [16384, 1], P(('enc', 'llm')), may hold values from 0 to 127; in each aligned block of 128 rows (0 to 127, 128 to 255, ...) at most 2 rows name the same one
- cotangent: bfloat16 [32768, 2048], P(('enc', 'llm')), may hold values from -6 to 6
Outputs:
- image_embeds: bfloat16 [32768, 2048], P(('enc', 'llm'))
- grad_w_in: float32 [5120, 5120], P('enc', 'llm')
- grad_w_out: float32 [5120, 2048], P('llm', 'enc')
- grad_patches: bfloat16 [16384, 5120], P('enc', 'llm')
Inputs may be any that keep to these rules, and one draw needn't show every extreme that they name: Among the 128 consecutive tokens of one aligned block, no owner is named more than 2 times, a bound that some block reaches.
All inputs are finite; a program needn't handle non-finite values.
Results may differ from a plain program's by a relative error of at most 0.018.
Values may be sent and summed in bfloat16 or wider, within the bound.
No kernel may reach another device: no remote copies, remote signals or barrier semaphores. Data moves between devices by JAX's collectives and lax.ppermute only.
A program may use at most 192 MiB of HBM per device.

v0:
```python
import jax
import jax.numpy as jnp
from jax import lax
from jax.sharding import PartitionSpec as P

VD = 1280
MERGE = 4
EPSILON = 1e-06
HALF_ROOT = 0.7071067811865476
DENSITY = 0.3989422804014327


def cut_along(shard, dim, devices):
    before, after = (shard.shape[:dim], shard.shape[dim + 1 :])
    return jnp.moveaxis(shard.reshape(*before, devices, -1, *after), dim, 0)


def sent_and_summed(shard, axis, dim):
    devices = lax.axis_size(axis)
    pieces = lax.all_to_all(cut_along(shard, dim, devices), axis, 0, 0, tiled=True)
    return jnp.sum(pieces.astype(jnp.float32), axis=0)


def in_order(pieces, dim):
    dims = list(pieces.shape[1:])
    dims[dim] *= pieces.shape[0]
    return jnp.moveaxis(pieces, 0, dim).reshape(dims)


def copy_for_each(shard, axis):
    devices = lax.axis_size(axis)
    return lax.all_to_all(
        jnp.broadcast_to(shard[None], (devices, *shard.shape)), axis, 0, 0, tiled=True
    )


def collect(shard, axis, dim):
    return in_order(copy_for_each(shard, axis), dim)


def gelu_slope(hidden):
    cdf = 0.5 * (1.0 + lax.erf(hidden * HALF_ROOT))
    return cdf + hidden * jnp.exp(-0.5 * hidden * hidden) * DENSITY


def local(patches, ln_gain, w_in, b_in, w_out, b_out, owner, cotangent):
    group_size = lax.axis_size("llm")
    enc_size = lax.axis_size("enc")
    devices = enc_size * group_size
    slot_cap = cotangent.shape[0] // devices
    gathered = lax.all_gather(patches, "llm", axis=1, tiled=True)
    tokens = gathered.shape[0]
    merged = gathered.astype(jnp.float32).reshape(tokens, MERGE, VD)
    inverse = lax.rsqrt(jnp.mean(merged * merged, axis=-1, keepdims=True) + EPSILON)
    normed = (
        (merged * inverse * ln_gain.astype(jnp.float32))
        .reshape(tokens, MERGE * VD)
        .astype(jnp.bfloat16)
    )
    hidden = jnp.dot(normed, w_in, preferred_element_type=jnp.float32) + b_in.astype(jnp.float32)
    active = jax.nn.gelu(hidden, approximate=False).astype(jnp.bfloat16)
    own_rows = tokens // group_size
    summed = sent_and_summed(
        jnp.dot(active, w_out, preferred_element_type=jnp.float32).astype(jnp.bfloat16), "llm", 0
    )
    embeds = (summed + b_out.astype(jnp.float32)).astype(jnp.bfloat16)
    targets = owner[:, 0]
    before = jnp.arange(own_rows)[:, None] > jnp.arange(own_rows)[None, :]
    same_owner = targets[:, None] == targets[None, :]
    rank_in = jnp.sum(jnp.logical_and(same_owner, before), axis=1)
    slot_ids = targets * slot_cap + rank_in
    placing = (
        jnp.arange(devices * slot_cap, dtype=jnp.int32)[:, None] == slot_ids[None, :]
    ).astype(jnp.bfloat16)
    outgoing = jnp.dot(placing, embeds, preferred_element_type=jnp.float32).astype(jnp.bfloat16)
    image_embeds = lax.all_to_all(outgoing, ("enc", "llm"), split_axis=0, concat_axis=0, tiled=True)
    returned = lax.all_to_all(cotangent, ("enc", "llm"), split_axis=0, concat_axis=0, tiled=True)
    own_grad = jnp.dot(placing.T, returned, preferred_element_type=jnp.float32).astype(jnp.bfloat16)
    grad_embeds = collect(own_grad, "llm", 0)
    grad_active = lax.dot_general(
        grad_embeds, w_out, (((1,), (1,)), ((), ())), preferred_element_type=jnp.float32
    )
    grad_hidden = (grad_active * gelu_slope(hidden)).astype(jnp.bfloat16)
    out_term = lax.dot_general(
        active, grad_embeds, (((0,), (0,)), ((), ())), preferred_element_type=jnp.float32
    )
    grad_w_out = lax.psum_scatter(
        out_term.astype(jnp.bfloat16), "enc", scatter_dimension=1, tiled=True
    ).astype(jnp.float32)
    grad_w_in = lax.psum_scatter(
        lax.dot_general(
            normed, grad_hidden, (((0,), (0,)), ((), ())), preferred_element_type=jnp.float32
        ).astype(jnp.bfloat16),
        "enc",
        scatter_dimension=0,
        tiled=True,
    ).astype(jnp.float32)
    feature_term = lax.dot_general(
        grad_hidden, w_in, (((1,), (1,)), ((), ())), preferred_element_type=jnp.float32
    )
    grad_normed = sent_and_summed(feature_term.astype(jnp.bfloat16), "llm", 1)
    own_count = patches.shape[1] // VD
    local_inverse = lax.dynamic_slice_in_dim(
        inverse, lax.axis_index("llm") * own_count, own_count, 1
    )
    local_x = patches.astype(jnp.float32).reshape(tokens, own_count, VD)
    scaled = grad_normed.reshape(tokens, own_count, VD) * ln_gain.astype(jnp.float32)
    projection = jnp.mean(scaled * local_x, axis=-1, keepdims=True)
    cubed = local_inverse * local_inverse * local_inverse
    grad_patches = (
        (local_inverse * scaled - local_x * cubed * projection)
        .reshape(tokens, own_count * VD)
        .astype(jnp.bfloat16)
    )
    return (image_embeds, grad_w_in, grad_w_out, grad_patches)


def solution(mesh):
    in_specs = (
        P("enc", "llm"),
        P(),
        P(None, "llm"),
        P("llm"),
        P("llm", None),
        P(),
        P(("enc", "llm"), None),
        P(("enc", "llm"), None),
    )
    out_specs = (P(("enc", "llm"), None), P("enc", "llm"), P("llm", "enc"), P("enc", "llm"))
    return jax.shard_map(local, mesh=mesh, in_specs=in_specs, out_specs=out_specs, check_vma=False)
```

profile of v0, /device:TPU:0, one launch (start us, length us, event | category | flops | bytes accessed | tf_op | source)
XLA Modules:
  0.0 377.8 jit_solution(15109931664863186243)
XLA Ops:
  7.2 0.0 all-gather.2.cloned.1.call-start
  7.2 0.7 all-gather.2.cloned.1.call-update
  7.9 2.5 all_to_all.29
  10.5 11.2 %all-to-all-start.2 = ((bf16[128,2,2048]{2,1,0:T(2,128)(2,1)}), bf16[128,2,2048]{2,1,0:T(2,128)(2,1)S(1)}, u32[]{:S(2)}, u32[]{:S(2)}) async-start(bf16[128,2,2048]{2,1,0:T(2,128)(2,1)} %all_to_all.29), calls=%async_computation.2 | async-start | bytes 2097152 | tf_op jit(solution)/shard_map/all_to_all | solution.py:77
  21.7 0.2 convert_reduce_fusion.2
  21.9 18.4 %all-to-all-done.2 = bf16[128,2,2048]{2,1,0:T(2,128)(2,1)S(1)} async-done(((bf16[128,2,2048]{2,1,0:T(2,128)(2,1)}), bf16[128,2,2048]{2,1,0:T(2,128)(2,1)S(1)}, u32[]{:S(2)}, u32[]{:S(2)}) %all-to-all-start.2) | async-done | bytes 1048608 | tf_op jit(solution)/shard_map/all_to_all | solution.py:77
  40.3 0.4 all_to_all.31
  40.7 0.4 convolution_convert_fusion.5
  41.1 1.6 broadcast_in_dim.2
  42.7 4.5 %all-to-all-start.3 = ((bf16[4,128,2048]{2,1,0:T(8,128)(2,1)}), bf16[4,128,2048]{2,1,0:T(8,128)(2,1)}, u32[]{:S(2)}, u32[]{:S(2)}) async-start(bf16[4,128,2048]{2,1,0:T(8,128)(2,1)} %broadcast_in_dim.2), calls=%async_computation.3 | async-start | bytes 4194304 | tf_op jit(solution)/shard_map/all_to_all | solution.py:32
  47.2 0.0 reduce-scatter.5.cloned.1.call-start
  47.2 53.2 %all-gather.2.cloned.1.call-done = bf16[512,5120]{1,0:T(8,128)(2,1)} async-done(((bf16[512,1280]{1,0:T(8,128)(2,1)}), bf16[512,5120]{1,0:T(8,128)(2,1)}) %all-gather.2.cloned.1.call-update) | async-done | bytes 5242896 | tf_op jit(solution)/shard_map/all_gather | solution.py:51
  100.4 7.8 %convert_multiply_fusion.1 = f32[512,5120]{1,0:T(8,128)} fusion(bf16[512,5120]{1,0:T(8,128)(2,1)} %all-gather.2.cloned.1.call-done), kind=kLoop, calls=%fused_computation.2 | loop fusion | flops 5242880 | bytes 15728640 | tf_op jit(solution)/shard_map/mul | solution.py:54
  108.2 13.6 %mul.129 = f32[512,4,1280]{2,1,0:T(4,128)} reshape(f32[512,5120]{1,0:T(8,128)} %convert_multiply_fusion.1) | data formatting | bytes 20971520 | tf_op jit(solution)/shard_map/mul | solution.py:54
  121.8 5.4 %reduce_sum.46 = f32[512,4]{1,0:T(8,128)S(1)} reduce(f32[512,4,1280]{2,1,0:T(4,128)} %mul.129, f32[]{:T(128)} %constant.40.clone.1), dimensions={2}, to_apply=%region_1.0 | reduce | flops 2619392 | bytes 10493956 | tf_op jit(solution)/shard_map/reduce_sum | solution.py:54
  127.3 1.4 mul.130
  128.7 6.3 %copy.17 = f32[64,8,4,1280]{3,1,2,0:T(8,128)} copy(f32[64,8,4,1280]{3,2,1,0:T(4,128)S(1)} %bitcast.29) | data formatting | bytes 20971520
  135.0 9.6 %fusion.1 = bf16[512,5120]{1,0:T(8,128)(2,1)} fusion(f32[512,5120]{1,0:T(8,128)} %bitcast.28, bf16[512,5120]{1,0:T(8,128)(2,1)} %all-gather.2.cloned.1.call-done, f32[5120]{0:T(1024)S(1)} %mul.134), kind=kLoop, calls=%fused_computation.4 | loop fusion | flops 10485760 | bytes 20992000 | tf_op jit(solution)/shard_map/convert_element_type | solution.py:58
  144.6 19.1 %fusion.9 = (bf16[512,1280]{1,0:T(8,128)(2,1)S(1)}, f32[512,1280]{1,0:T(8,128)}) fusion(f32[1280]{0:T(1024)S(1)} %convert_element_type.69, bf16[512,5120]{1,0:T(8,128)(2,1)} %fusion.1, bf16[5120,1280]{1,0:T(8,128)(2,1)} %param.10), kind=kOutput, calls=%fused_computation.24 | convolution fusion | flops 6754140160 | bytes 22287360 | tf_op jit(solution)/shard_map/dot_general | solution.py:60
  163.7 6.8 %convolution_convert_fusion.1 = bf16[1280,2048]{0,1:T(8,128)(2,1)} fusion(bf16[512,1280]{1,0:T(8,128)(2,1)S(1)} %get-tuple-element.4, bf16[512,2048]{1,0:T(8,128)(2,1)} %bitcast.2), kind=kOutput, calls=%fused_computation.6 | convolution fusion | flops 2686976000 | bytes 8650752 | tf_op jit(solution)/shard_map/dot_general | solution.py:84
  170.5 0.0 reduce-scatter.5.cloned.1.call-update
  170.5 0.3 reduce-scatter.3.cloned.1.call-start
  170.8 7.5 %fusion.2 = bf16[512,1280]{1,0:T(8,128)(2,1)S(1)} fusion(bf16[512,2048]{1,0:T(8,128)(2,1)} %bitcast.2, bf16[1280,2048]{1,0:T(8,128)(2,1)} %param.12, f32[512,1280]{1,0:T(8,128)} %get-tuple-element.5), kind=kOutput, calls=%fused_computation.16 | convolution fusion | flops 2690908160 | bytes 11272192 | tf_op jit(solution)/shard_map/dot_general | solution.py:80
  178.3 0.0 copy-start.5
  178.3 1.0 copy-done.5
  179.4 10.0 %convolution_convert_fusion = bf16[5120,1280]{1,0:T(8,128)(2,1)} fusion(bf16[512,5120]{1,0:T(8,128)(2,1)S(1)} %bitcast.33, bf16[512,1280]{1,0:T(8,128)(2,1)S(1)} %fusion.2), kind=kOutput, calls=%fused_computation | convolution fusion | flops 6717440000 | bytes 19660800 | tf_op jit(solution)/shard_map/dot_general | solution.py:91
  189.4 0.0 reduce-scatter.3.cloned.1.call-update
  189.4 6.7 %convolution_convert_fusion.3 = bf16[512,2048]{1,0:T(8,128)(2,1)} fusion(bf16[512,1280]{1,0:T(8,128)(2,1)S(1)} %get-tuple-element.4, bf16[1280,2048]{1,0:T(8,128)(2,1)} %param.12), kind=kOutput, calls=%fused_computation.17 | convolution fusion | flops 2685403136 | bytes 8650752 | tf_op jit(solution)/shard_map/dot_general | solution.py:64
  196.2 3.8 all-to-all-start
  200.0 26.7 %all-to-all-done = bf16[4,128,2048]{2,1,0:T(8,128)(2,1)S(1)} async-done(((bf16[4,128,2048]{2,1,0:T(8,128)(2,1)}), bf16[4,128,2048]{2,1,0:T(8,128)(2,1)S(1)}, u32[]{:S(2)}, u32[]{:S(2)}) %all-to-all-start) | async-done | bytes 2097184 | tf_op jit(solution)/shard_map/all_to_all | solution.py:20
  226.7 0.4 convert_reduce_fusion.1
  227.1 0.4 convolution_convert_fusion.4
  227.5 0.0 copy-start.6
  227.5 1.5 all_to_all.26
  229.0 8.7 %all-to-all-start.1 = ((bf16[128,2,2048]{2,1,0:T(2,128)(2,1)}), bf16[128,2,2048]{2,1,0:T(2,128)(2,1)S(1)}, u32[]{:S(2)}, u32[]{:S(2)}) async-start(bf16[128,2,2048]{2,1,0:T(2,128)(2,1)} %all_to_all.26), calls=%async_computation.1 | async-start | bytes 2097152 | tf_op jit(solution)/shard_map/all_to_all | solution.py:76
  237.8 13.5 %convolution_convert_fusion.2 = bf16[512,5120]{1,0:T(8,128)(2,1)} fusion(bf16[512,1280]{1,0:T(8,128)(2,1)S(1)} %copy-done.6, bf16[5120,1280]{1,0:T(8,128)(2,1)} %param.10), kind=kOutput, calls=%fused_computation.7 | convolution fusion | flops 6713507840 | bytes 19660800 | tf_op jit(solution)/shard_map/dot_general | solution.py:98
  251.2 5.1 %copy.19 = bf16[64,4,8,1280]{3,2,0,1:T(8,128)(2,1)} copy(bf16[64,4,8,1280]{3,2,1,0:T(8,128)(2,1)} %bitcast.31) | data formatting | bytes 10485760 | tf_op jit(solution)/shard_map/reshape | solution.py:15
  256.4 0.8 all-to-all-done.1
  257.2 5.2 %all-to-all-start.4 = ((bf16[4,512,1280]{2,1,0:T(8,128)(2,1)}), bf16[4,512,1280]{2,1,0:T(8,128)(2,1)}, u32[]{:S(2)}, u32[]{:S(2)}) async-start(bf16[4,512,1280]{2,1,0:T(8,128)(2,1)} %bitcast.30), calls=%async_computation.6 | async-start | bytes 10485760 | tf_op jit(solution)/shard_map/all_to_all | solution.py:20
  262.3 0.2 dynamic-slice_reduce_fusion
  262.6 1.2 all_to_all.28
  263.8 59.2 %all-to-all-done.4 = bf16[4,512,1280]{2,1,0:T(8,128)(2,1)} async-done(((bf16[4,512,1280]{2,1,0:T(8,128)(2,1)}), bf16[4,512,1280]{2,1,0:T(8,128)(2,1)}, u32[]{:S(2)}, u32[]{:S(2)}) %all-to-all-start.4) | async-done | bytes 5242912 | tf_op jit(solution)/shard_map/all_to_all | solution.py:20
  323.0 3.7 convert_reduce_fusion
  326.7 0.5 fusion.6
  327.1 1.7 fusion.5
  328.8 1.7 convert_element_type.81
  330.5 38.8 %reduce-scatter.3.cloned.1.call-done = bf16[160,1280]{1,0:T(8,128)(2,1)} async-done(((bf16[5120,1280]{1,0:T(8,128)(2,1)}), bf16[160,1280]{1,0:T(8,128)(2,1)}) %reduce-scatter.3.cloned.1.call-update) | async-done | bytes 409616 | tf_op jit(solution)/shard_map/reduce_scatter | solution.py:90
  369.3 1.9 convert_element_type.79
  (27 shorter events, 0.1 us)
Async XLA Ops:
  7.2 14.5 %copy-start.1 = (bf16[1280]{0:T(1024)(128)(2,1)S(1)}, bf16[1280]{0:T(1024)(128)(2,1)}, u32[]{:S(2)}) copy-start(bf16[1280]{0:T(1024)(128)(2,1)} %param.9) | copy-start | bytes 7684
  7.2 14.5 %copy-start.2 = (bf16[1280]{0:T(1024)(128)(2,1)S(1)}, bf16[1280]{0:T(1024)(128)(2,1)}, u32[]{:S(2)}) copy-start(bf16[1280]{0:T(1024)(128)(2,1)} %param.11) | copy-start | bytes 7684
  7.2 14.5 %copy-start.4 = (s32[128,1]{0,1:T(1,128)S(1)}, s32[128,1]{0,1:T(1,128)}, u32[]{:S(2)}) copy-start(s32[128,1]{0,1:T(1,128)} %param.14) | copy-start | bytes 1540
  7.2 93.2 %all-gather.2.cloned.1.call-start = ((), (), s32[]{:S(2)}) async-start(), calls=%async_computation.7 | async-start | bytes 6553600 | tf_op jit(solution)/shard_map/all_gather | solution.py:51
  10.5 29.8 %all-to-all-start.2 = ((bf16[128,2,2048]{2,1,0:T(2,128)(2,1)}), bf16[128,2,2048]{2,1,0:T(2,128)(2,1)S(1)}, u32[]{:S(2)}, u32[]{:S(2)}) async-start(bf16[128,2,2048]{2,1,0:T(2,128)(2,1)} %all_to_all.29), calls=%async_computation.2 | async-start | bytes 2097152 | tf_op jit(solution)/shard_map/all_to_all | solution.py:77
  42.7 121.0 %all-to-all-start.3 = ((bf16[4,128,2048]{2,1,0:T(8,128)(2,1)}), bf16[4,128,2048]{2,1,0:T(8,128)(2,1)}, u32[]{:S(2)}, u32[]{:S(2)}) async-start(bf16[4,128,2048]{2,1,0:T(8,128)(2,1)} %broadcast_in_dim.2), calls=%async_computation.3 | async-start | bytes 4194304 | tf_op jit(solution)/shard_map/all_to_all | solution.py:32
  47.2 281.7 %reduce-scatter.5.cloned.1.call-start = ((), (), s32[]{:S(2)}) async-start(), calls=%async_computation.9 | async-start | bytes 5406720 | tf_op jit(solution)/shard_map/reduce_scatter | solution.py:87
  170.5 8.9 %slice-start = ((s8[5242880]{0:T(1024)(128)(4,1)}), s8[1048576]{0:T(1024)(128)(4,1)S(1)}, s32[]{:S(2)}) async-start(s8[5242880]{0:T(1024)(128)(4,1)} %bitcast.32), calls=%async_computation.10 | async-start | bytes 2097152
  170.5 198.8 %reduce-scatter.3.cloned.1.call-start = ((), (), s32[]{:S(2)}) async-start(), calls=%async_computation.8 | async-start | bytes 13516800 | tf_op jit(solution)/shard_map/reduce_scatter | solution.py:90
  170.8 8.6 %slice-start.1 = ((s8[5242880]{0:T(1024)(128)(4,1)}), s8[4194304]{0:T(1024)(128)(4,1)S(1)}, s32[]{:S(2)}) async-start(s8[5242880]{0:T(1024)(128)(4,1)} %bitcast.32), calls=%async_computation.11 | async-start | bytes 8388608
  178.3 1.1 copy-start.5
  196.2 3.8 copy-start.3
  196.2 30.5 %all-to-all-start = ((bf16[4,128,2048]{2,1,0:T(8,128)(2,1)}), bf16[4,128,2048]{2,1,0:T(8,128)(2,1)S(1)}, u32[]{:S(2)}, u32[]{:S(2)}) async-start(bf16[4,128,2048]{2,1,0:T(8,128)(2,1)} %bitcast.34), calls=%async_computation | async-start | bytes 4194304 | tf_op jit(solution)/shard_map/all_to_all | solution.py:20
  227.5 10.2 %copy-start.6 = (bf16[512,1280]{1,0:T(8,128)(2,1)S(1)}, bf16[512,1280]{1,0:T(8,128)(2,1)}, u32[]{:S(2)}) copy-start(bf16[512,1280]{1,0:T(8,128)(2,1)} %copy-done.5) | copy-start | bytes 3932164
  229.0 28.1 %all-to-all-start.1 = ((bf16[128,2,2048]{2,1,0:T(2,128)(2,1)}), bf16[128,2,2048]{2,1,0:T(2,128)(2,1)S(1)}, u32[]{:S(2)}, u32[]{:S(2)}) async-start(bf16[128,2,2048]{2,1,0:T(2,128)(2,1)} %all_to_all.26), calls=%async_computation.1 | async-start | bytes 2097152 | tf_op jit(solution)/shard_map/all_to_all | solution.py:76
  257.2 65.8 %all-to-all-start.4 = ((bf16[4,512,1280]{2,1,0:T(8,128)(2,1)}), bf16[4,512,1280]{2,1,0:T(8,128)(2,1)}, u32[]{:S(2)}, u32[]{:S(2)}) async-start(bf16[4,512,1280]{2,1,0:T(8,128)(2,1)} %bitcast.30), calls=%async_computation.6 | async-start | bytes 10485760 | tf_op jit(solution)/shard_map/all_to_all | solution.py:20
  263.8 62.9 %copy-start = (bf16[512,1280]{1,0:T(8,128)(2,1)S(1)}, bf16[512,1280]{1,0:T(8,128)(2,1)}, u32[]{:S(2)}) copy-start(bf16[512,1280]{1,0:T(8,128)(2,1)} %param.8) | copy-start | bytes 3932164
Sparse Core Ops, SparseCore 0:
  9.7 90.7 all-gather.1
  170.6 90.3 reduce-scatter.4
  264.9 104.3 reduce-scatter.2
where the time goes:
time: 379 us; the launch traced here: 378 us
  waiting for transfers between devices  198 us (52%)
  matrix products  64.4 us (17%)
  local copies, waits for them, and re-layouts  35 us (9%)
  starting transfers between devices  33.6 us (9%)
  other arithmetic  32.9 us (9%)
  between operations  14 us (4%)
    all_to_all x2, waiting for transfers between devices, sent_and_summed(): lax.all_to_all(cut_along(shard, dim, devices), axis, 0, 0, tiled=True)  85.9 us
    all_gather x1, waiting for transfers between devices, local(): gathered = lax.all_gather(patches, 'llm', axis=1, tiled=True)  53.2 us
    reduce_scatter x1, waiting for transfers between devices, local(): lax.psum_scatter(lax.dot_general(normed, grad_hidden, (((0,), (0,)), ((),...  38.8 us
    dot_general x1, matrix products, local(): jnp.dot(normed, w_in, preferred_element_type=jnp.float32)  19.1 us
    all_to_all x1, waiting for transfers between devices, local(): lax.all_to_all(cotangent, ('enc', 'llm'), split_axis=0, concat_axis=0, ti...  18.4 us
    mul x1, local copies, waits for them, and re-layouts, local(): merged * merged  13.6 us
    dot_general x1, matrix products, local(): lax.dot_general(grad_hidden, w_in, (((1,), (1,)), ((), ())), preferred_el...  13.5 us
    all_to_all x1, starting transfers between devices, local(): lax.all_to_all(cotangent, ('enc', 'llm'), split_axis=0, concat_axis=0, ti...  11.2 us
  transfers between devices with their start and end apart: 8, of which 6 were waited for; matrix products, arithmetic and copies ran while one was open for 31% of the time, Pallas kernels for 0%

commit v1 on v0

--- a/solution.py
+++ b/solution.py
@@ -8,6 +8,14 @@
 EPSILON = 1e-06
 HALF_ROOT = 0.7071067811865476
 DENSITY = 0.3989422804014327
+
+
+def gather_from_all(array, axis, dim):
+    length = lax.axis_size(axis)
+    repeats = [length if d == dim else 1 for d in range(array.ndim)]
+    return lax.all_to_all(
+        jnp.tile(array, repeats), axis, split_axis=dim, concat_axis=dim, tiled=True
+    )
 
 
 def cut_along(shard, dim, devices):
@@ -48,7 +56,7 @@
     enc_size = lax.axis_size("enc")
     devices = enc_size * group_size
     slot_cap = cotangent.shape[0] // devices
-    gathered = lax.all_gather(patches, "llm", axis=1, tiled=True)
+    gathered = gather_from_all(patches, "llm", 1)
     tokens = gathered.shape[0]
     merged = gathered.astype(jnp.float32).reshape(tokens, MERGE, VD)
     inverse = lax.rsqrt(jnp.mean(merged * merged, axis=-1, keepdims=True) + EPSILON)

time: 379 us -> 358 us (0.945)
  blocking collectives: 0 us -> 29.6 us
  other arithmetic: 32.9 us -> 14.9 us
  waiting for transfers between devices: 198 us -> 184 us
  starting transfers between devices: 33.6 us -> 23.9 us
  local copies, waits for them, and re-layouts: 35 us -> 27.4 us
    all_gather x1 -> x0, waiting for transfers between devices: 53.2 us -> none  [local(): gathered = lax.all_gather(patches, 'llm', axis=1, tiled=True)]
    all_to_all x1, waiting for transfers between devices: 18.4 us -> 59.6 us  [gather_from_all(): lax.all_to_all(jnp.tile(array, repeats), axis, split_axis=dim, concat_axi...]
    all_to_all x0 -> x1, blocking collectives: none -> 29.6 us  [local(): lax.all_to_all(cotangent, ('enc', 'llm'), split_axis=0, concat_axis=0, ti...]
    mul x4 -> x0, local copies, waits for them, and re-layouts: 15 us -> none  [the longest x1 13.6 us: local(): merged * merged]
    convert_element_type x1, other arithmetic: 9.63 us -> 1.23 us  [local(): normed = (merged * inverse * ln_gain.astype(jnp.float32)).reshape(tokens,...]
    all_to_all x0 -> x1, local copies, waits for them, and re-layouts: none -> 7.89 us  [gather_from_all(): lax.all_to_all(jnp.tile(array, repeats), axis, split_axis=dim, concat_axi...]
    mul x1 -> x0, other arithmetic: 7.78 us -> none  [local(): merged * merged]
    all_to_all x1, starting transfers between devices: 11.2 us -> 5.2 us  [gather_from_all(): lax.all_to_all(jnp.tile(array, repeats), axis, split_axis=dim, concat_axi...]
  transfers between devices with their start and end apart: 8 -> 7, of which waited for: 6 -> 5; matrix products, arithmetic and copies ran while one was open for 31% -> 23% of each run, Pallas kernels for 0% -> 0%
where the time goes in v1:
time: 358 us; the launch traced here: 357 us
  waiting for transfers between devices  184 us (51%)
  matrix products  63.3 us (18%)
  blocking collectives  29.6 us (8%)
  local copies, waits for them, and re-layouts  27.4 us (8%)
  starting transfers between devices  23.9 us (7%)
  other arithmetic  14.9 us (4%)
  between operations  14.2 us (4%)
    all_to_all x2, waiting for transfers between devices, sent_and_summed(): lax.all_to_all(cut_along(shard, dim, devices), axis, 0, 0, tiled=True)  84.9 us
    all_to_all x1, waiting for transfers between devices, gather_from_all(): lax.all_to_all(jnp.tile(array, repeats), axis, split_axis=dim, concat_axi...  59.6 us
    reduce_scatter x1, waiting for transfers between devices, local(): lax.psum_scatter(lax.dot_general(normed, grad_hidden, (((0,), (0,)), ((),...  38.8 us
    all_to_all x1, blocking collectives, local(): lax.all_to_all(cotangent, ('enc', 'llm'), split_axis=0, concat_axis=0, ti...  29.6 us
    dot_general x1, matrix products, local(): jnp.dot(normed, w_in, preferred_element_type=jnp.float32)  18 us
    dot_general x1, matrix products, local(): lax.dot_general(grad_hidden, w_in, (((1,), (1,)), ((), ())), preferred_el...  13.7 us
    dot_general x1, matrix products, local(): lax.dot_general(normed, grad_hidden, (((0,), (0,)), ((), ())), preferred_...  9.89 us
    all_to_all x2, starting transfers between devices, sent_and_summed(): lax.all_to_all(cut_along(shard, dim, devices), axis, 0, 0, tiled=True)  9.7 us
  transfers between devices with their start and end apart: 7, of which 5 were waited for; matrix products, arithmetic and copies ran while one was open for 23% of the time, Pallas kernels for 0%

profile of v1, /device:TPU:0, one launch (start us, length us, event | category | flops | bytes accessed | tf_op | source)
XLA Modules:
  0.0 357.3 jit_solution(6705087031440137952)
XLA Ops:
  7.2 0.0 copy-start.1
  7.2 1.9 all_to_all.34
  9.0 29.6 %all_to_all.45 = bf16[128,2,2048]{2,1,0:T(2,128)(2,1)S(1)} all-to-all(bf16[128,2,2048]{2,1,0:T(2,128)(2,1)S(1)} %all_to_all.34), channel_id=1, replica_groups=mesh['enc'=32,'llm'=4] {'enc','llm'}, dimensions={0} | all-to-all | bytes 2097152 | tf_op jit(solution)/shard_map/all_to_all | solution.py:85
  38.6 2.7 tile.2
  41.3 5.2 %all-to-all-start = ((bf16[512,4,1280]{2,0,1:T(8,128)(2,1)}), bf16[512,4,1280]{2,0,1:T(8,128)(2,1)}, u32[]{:S(2)}, u32[]{:S(2)}) async-start(bf16[512,4,1280]{2,0,1:T(8,128)(2,1)} %tile.2), calls=%async_computation | async-start | bytes 10485760 | tf_op jit(solution)/shard_map/all_to_all | solution.py:16
  46.6 0.0 copy-done.5
  46.6 0.2 convert_reduce_fusion.2
  46.8 0.4 all_to_all.36
  47.2 0.4 convolution_convert_fusion.5
  47.6 59.6 %all-to-all-done = bf16[512,4,1280]{2,0,1:T(8,128)(2,1)} async-done(((bf16[512,4,1280]{2,0,1:T(8,128)(2,1)}), bf16[512,4,1280]{2,0,1:T(8,128)(2,1)}, u32[]{:S(2)}, u32[]{:S(2)}) %all-to-all-start) | async-done | bytes 5242912 | tf_op jit(solution)/shard_map/all_to_all | solution.py:16
  107.2 1.6 broadcast_in_dim.2
  108.8 3.6 %all-to-all-start.4 = ((bf16[4,128,2048]{2,1,0:T(8,128)(2,1)}), bf16[4,128,2048]{2,1,0:T(8,128)(2,1)S(1)}, u32[]{:S(2)}, u32[]{:S(2)}) async-start(bf16[4,128,2048]{2,1,0:T(8,128)(2,1)} %broadcast_in_dim.2), calls=%async_computation.4 | async-start | bytes 4194304 | tf_op jit(solution)/shard_map/all_to_all | solution.py:40
  112.4 0.2 reduce-scatter.5.cloned.1.call-start
  112.6 7.9 %copy.16 = bf16[512,4,1280]{0,2,1:T(8,128)(2,1)} copy(bf16[512,4,1280]{2,0,1:T(8,128)(2,1)} %all-to-all-done) | data formatting | bytes 10485760 | tf_op jit(solution)/shard_map/all_to_all | solution.py:16
  120.5 3.7 %fusion = f32[512,4]{0,1:T(4,128)S(1)} fusion(bf16[512,4,1280]{0,2,1:T(8,128)(2,1)} %copy.16), kind=kLoop, calls=%fused_computation.3 | loop fusion | flops 7862272 | bytes 5251072 | tf_op jit(solution)/shard_map/reduce_sum | solution.py:62
  124.2 0.4 copy-done
  124.6 1.2 fusion.2
  125.8 2.3 copy-done.2
  128.1 18.0 %fusion.10 = (bf16[512,1280]{1,0:T(8,128)(2,1)}, f32[512,1280]{1,0:T(8,128)}) fusion(f32[1280]{0:T(1024)S(1)} %convert_element_type.74, bf16[512,5120]{0,1:T(8,128)(2,1)S(1)} %bitcast.30, bf16[5120,1280]{1,0:T(8,128)(2,1)} %param.10), kind=kOutput, calls=%fused_computation.25 | convolution fusion | flops 6754140160 | bytes 22287360 | tf_op jit(solution)/shard_map/dot_general | solution.py:68
  146.1 0.0 all-to-all-done.4
  146.1 6.7 %convolution_convert_fusion.1 = bf16[1280,2048]{0,1:T(8,128)(2,1)} fusion(bf16[512,1280]{1,0:T(8,128)(2,1)} %get-tuple-element.6, bf16[512,2048]{1,0:T(8,128)(2,1)S(1)} %bitcast.35), kind=kOutput, calls=%fused_computation.7 | convolution fusion | flops 2686976000 | bytes 8650752 | tf_op jit(solution)/shard_map/dot_general | solution.py:92
  152.9 0.0 reduce-scatter.5.cloned.1.call-update
  152.9 0.3 reduce-scatter.3.cloned.1.call-start
  153.1 0.0 slice-start.1
  153.2 7.5 %fusion.3 = bf16[512,1280]{1,0:T(8,128)(2,1)S(1)} fusion(bf16[512,2048]{1,0:T(8,128)(2,1)} %bitcast.36, bf16[1280,2048]{1,0:T(8,128)(2,1)} %param.12, f32[512,1280]{1,0:T(8,128)} %get-tuple-element.7), kind=kOutput, calls=%fused_computation.17 | convolution fusion | flops 2690908160 | bytes 11272192 | tf_op jit(solution)/shard_map/dot_general | solution.py:88
  160.7 1.1 copy-done.9
  161.7 9.9 %convolution_convert_fusion = bf16[5120,1280]{1,0:T(8,128)(2,1)} fusion(bf16[512,5120]{0,1:T(8,128)(2,1)S(1)} %bitcast.33, bf16[512,1280]{1,0:T(8,128)(2,1)S(1)} %fusion.3), kind=kOutput, calls=%fused_computation | convolution fusion | flops 6717440000 | bytes 19660800 | tf_op jit(solution)/shard_map/dot_general | solution.py:99
  171.6 0.0 reduce-scatter.3.cloned.1.call-update
  171.7 1.3 copy-done.8
  173.0 6.7 %convolution_convert_fusion.3 = bf16[512,2048]{1,0:T(8,128)(2,1)} fusion(bf16[512,1280]{1,0:T(8,128)(2,1)S(1)} %copy-done.8, bf16[1280,2048]{1,0:T(8,128)(2,1)} %param.12), kind=kOutput, calls=%fused_computation.18 | convolution fusion | flops 2685403136 | bytes 8650752 | tf_op jit(solution)/shard_map/dot_general | solution.py:72
  179.7 4.6 %all-to-all-start.1 = ((bf16[4,128,2048]{2,1,0:T(8,128)(2,1)}), bf16[4,128,2048]{2,1,0:T(8,128)(2,1)S(1)}, u32[]{:S(2)}, u32[]{:S(2)}) async-start(bf16[4,128,2048]{2,1,0:T(8,128)(2,1)} %bitcast.37), calls=%async_computation.1 | async-start | bytes 4194304 | tf_op jit(solution)/shard_map/all_to_all | solution.py:28
  184.4 25.5 %all-to-all-done.1 = bf16[4,128,2048]{2,1,0:T(8,128)(2,1)S(1)} async-done(((bf16[4,128,2048]{2,1,0:T(8,128)(2,1)}), bf16[4,128,2048]{2,1,0:T(8,128)(2,1)S(1)}, u32[]{:S(2)}, u32[]{:S(2)}) %all-to-all-start.1) | async-done | bytes 2097184 | tf_op jit(solution)/shard_map/all_to_all | solution.py:28
  209.8 0.4 convert_reduce_fusion.1
  210.2 0.4 convolution_convert_fusion.4
  210.7 1.5 all_to_all.31
  212.2 4.9 %all-to-all-start.2 = ((bf16[128,2,2048]{2,1,0:T(2,128)(2,1)}), bf16[128,2,2048]{2,1,0:T(2,128)(2,1)S(1)}, u32[]{:S(2)}, u32[]{:S(2)}) async-start(bf16[128,2,2048]{2,1,0:T(2,128)(2,1)} %all_to_all.31), calls=%async_computation.2 | async-start | bytes 2097152 | tf_op jit(solution)/shard_map/all_to_all | solution.py:84
  217.1 13.7 %convolution_convert_fusion.2 = bf16[512,5120]{1,0:T(8,128)(2,1)} fusion(bf16[512,1280]{1,0:T(8,128)(2,1)} %copy-done.9, bf16[5120,1280]{1,0:T(8,128)(2,1)} %param.10), kind=kOutput, calls=%fused_computation.8 | convolution fusion | flops 6713507840 | bytes 19660800 | tf_op jit(solution)/shard_map/dot_general | solution.py:106
  230.7 5.1 %copy.20 = bf16[64,4,8,1280]{3,2,0,1:T(8,128)(2,1)} copy(bf16[64,4,8,1280]{3,2,1,0:T(8,128)(2,1)} %bitcast.34) | data formatting | bytes 10485760 | tf_op jit(solution)/shard_map/reshape | solution.py:23
  235.9 0.5 all-to-all-done.2
  236.4 5.1 %all-to-all-start.5 = ((bf16[4,512,1280]{2,1,0:T(8,128)(2,1)}), bf16[4,512,1280]{2,1,0:T(8,128)(2,1)}, u32[]{:S(2)}, u32[]{:S(2)}) async-start(bf16[4,512,1280]{2,1,0:T(8,128)(2,1)} %bitcast.29), calls=%async_computation.7 | async-start | bytes 10485760 | tf_op jit(solution)/shard_map/all_to_all | solution.py:28
  241.5 1.2 all_to_all.33
  242.7 59.5 %all-to-all-done.5 = bf16[4,512,1280]{2,1,0:T(8,128)(2,1)} async-done(((bf16[4,512,1280]{2,1,0:T(8,128)(2,1)}), bf16[4,512,1280]{2,1,0:T(8,128)(2,1)}, u32[]{:S(2)}, u32[]{:S(2)}) %all-to-all-start.5) | async-done | bytes 5242912 | tf_op jit(solution)/shard_map/all_to_all | solution.py:28
  302.2 3.7 %convert_reduce_fusion = f32[512,1280]{1,0:T(8,128)S(1)} fusion(bf16[4,512,1280]{2,1,0:T(8,128)(2,1)} %all-to-all-done.5), kind=kLoop, calls=%fused_computation.6 | loop fusion | flops 4587520 | bytes 7864320 | tf_op jit(solution)/shard_map/reduce_sum | solution.py:29
  305.9 0.5 fusion.7
  306.4 1.7 fusion.6
  308.0 1.7 convert_element_type.86
  309.7 38.8 %reduce-scatter.3.cloned.1.call-done = bf16[160,1280]{1,0:T(8,128)(2,1)} async-done(((bf16[5120,1280]{1,0:T(8,128)(2,1)}), bf16[160,1280]{1,0:T(8,128)(2,1)}) %reduce-scatter.3.cloned.1.call-update) | async-done | bytes 409616 | tf_op jit(solution)/shard_map/reduce_scatter | solution.py:98
  348.6 1.9 convert_element_type.84
  (26 shorter events, 0.1 us)
Async XLA Ops:
  7.2 31.5 %copy-start.1 = (bf16[512,1280]{1,0:T(8,128)(2,1)S(1)}, bf16[512,1280]{1,0:T(8,128)(2,1)}, u32[]{:S(2)}) copy-start(bf16[512,1280]{1,0:T(8,128)(2,1)} %param.8) | copy-start | bytes 3932164
  41.3 5.2 %copy-start.4 = (bf16[1280]{0:T(1024)(128)(2,1)S(1)}, bf16[1280]{0:T(1024)(128)(2,1)}, u32[]{:S(2)}) copy-start(bf16[1280]{0:T(1024)(128)(2,1)} %param.9) | copy-start | bytes 7684
  41.3 5.2 %copy-start.5 = (bf16[1280]{0:T(1024)(128)(2,1)S(1)}, bf16[1280]{0:T(1024)(128)(2,1)}, u32[]{:S(2)}) copy-start(bf16[1280]{0:T(1024)(128)(2,1)} %param.11) | copy-start | bytes 7684
  41.3 5.3 %copy-start.7 = (s32[128,1]{0,1:T(1,128)S(1)}, s32[128,1]{0,1:T(1,128)}, u32[]{:S(2)}) copy-start(s32[128,1]{0,1:T(1,128)} %param.14) | copy-start | bytes 1540
  41.3 65.9 %all-to-all-start = ((bf16[512,4,1280]{2,0,1:T(8,128)(2,1)}), bf16[512,4,1280]{2,0,1:T(8,128)(2,1)}, u32[]{:S(2)}, u32[]{:S(2)}) async-start(bf16[512,4,1280]{2,0,1:T(8,128)(2,1)} %tile.2), calls=%async_computation | async-start | bytes 10485760 | tf_op jit(solution)/shard_map/all_to_all | solution.py:16
  108.8 37.3 %all-to-all-start.4 = ((bf16[4,128,2048]{2,1,0:T(8,128)(2,1)}), bf16[4,128,2048]{2,1,0:T(8,128)(2,1)S(1)}, u32[]{:S(2)}, u32[]{:S(2)}) async-start(bf16[4,128,2048]{2,1,0:T(8,128)(2,1)} %broadcast_in_dim.2), calls=%async_computation.4 | async-start | bytes 4194304 | tf_op jit(solution)/shard_map/all_to_all | solution.py:40
  112.4 195.6 %reduce-scatter.5.cloned.1.call-start = ((), (), s32[]{:S(2)}) async-start(), calls=%async_computation.9 | async-start | bytes 5406720 | tf_op jit(solution)/shard_map/reduce_scatter | solution.py:95
  120.5 4.0 %copy-start = (bf16[512,4,1280]{0,2,1:T(8,128)(2,1)S(1)}, bf16[512,4,1280]{0,2,1:T(8,128)(2,1)}, u32[]{:S(2)}) copy-start(bf16[512,4,1280]{0,2,1:T(8,128)(2,1)} %copy.16) | copy-start | bytes 15728644
  125.8 2.3 copy-start.2
  146.1 6.7 %copy-start.3 = (bf16[4,128,2048]{2,1,0:T(8,128)(2,1)}, bf16[4,128,2048]{2,1,0:T(8,128)(2,1)S(1)}, u32[]{:S(2)}) copy-start(bf16[4,128,2048]{2,1,0:T(8,128)(2,1)S(1)} %all-to-all-done.4) | copy-start | bytes 6291460
  152.8 8.9 %slice-start = ((s8[5242880]{0:T(1024)(128)(4,1)}), s8[1048576]{0:T(1024)(128)(4,1)S(1)}, s32[]{:S(2)}) async-start(s8[5242880]{0:T(1024)(128)(4,1)} %bitcast.31), calls=%async_computation.10 | async-start | bytes 2097152
  152.9 195.7 %reduce-scatter.3.cloned.1.call-start = ((), (), s32[]{:S(2)}) async-start(), calls=%async_computation.8 | async-start | bytes 13516800 | tf_op jit(solution)/shard_map/reduce_scatter | solution.py:98
  153.1 8.6 %slice-start.1 = ((s8[5242880]{0:T(1024)(128)(4,1)}), s8[4194304]{0:T(1024)(128)(4,1)S(1)}, s32[]{:S(2)}) async-start(s8[5242880]{0:T(1024)(128)(4,1)} %bitcast.31), calls=%async_computation.11 | async-start | bytes 8388608
  160.7 1.1 copy-start.9
  171.6 1.4 copy-start.8
  179.7 4.7 %copy-start.6 = (bf16[2048]{0:T(1024)(128)(2,1)S(1)}, bf16[2048]{0:T(1024)(128)(2,1)}, u32[]{:S(2)}) copy-start(bf16[2048]{0:T(1024)(128)(2,1)} %param.13) | copy-start | bytes 12292
  179.7 30.1 %all-to-all-start.1 = ((bf16[4,128,2048]{2,1,0:T(8,128)(2,1)}), bf16[4,128,2048]{2,1,0:T(8,128)(2,1)S(1)}, u32[]{:S(2)}, u32[]{:S(2)}) async-start(bf16[4,128,2048]{2,1,0:T(8,128)(2,1)} %bitcast.37), calls=%async_computation.1 | async-start | bytes 4194304 | tf_op jit(solution)/shard_map/all_to_all | solution.py:28
  212.2 24.3 %all-to-all-start.2 = ((bf16[128,2,2048]{2,1,0:T(2,128)(2,1)}), bf16[128,2,2048]{2,1,0:T(2,128)(2,1)S(1)}, u32[]{:S(2)}, u32[]{:S(2)}) async-start(bf16[128,2,2048]{2,1,0:T(2,128)(2,1)} %all_to_all.31), calls=%async_computation.2 | async-start | bytes 2097152 | tf_op jit(solution)/shard_map/all_to_all | solution.py:84
  236.4 65.8 %all-to-all-start.5 = ((bf16[4,512,1280]{2,1,0:T(8,128)(2,1)}), bf16[4,512,1280]{2,1,0:T(8,128)(2,1)}, u32[]{:S(2)}, u32[]{:S(2)}) async-start(bf16[4,512,1280]{2,1,0:T(8,128)(2,1)} %bitcast.29), calls=%async_computation.7 | async-start | bytes 10485760 | tf_op jit(solution)/shard_map/all_to_all | solution.py:28
Sparse Core Ops, SparseCore 0:
  153.0 87.3 reduce-scatter.4
  244.3 104.2 reduce-scatter.2
